TPU v7x, 32 devices: a whole 2x2x4 slice. The times are simulated.
32 devices in a mesh: dp: 8 (over z, y), query: 4 (over x, core).
Axes of the slice: x: 2, y: 2, z: 4, core: 2. Of those that a mesh axis runs over, the one named last changes fastest.
Arguments:
- sensors: bfloat16 [3072, 4096], P('dp'), may hold values from -8 to 8
- query_index: int32 [2, 8192], P(None, 'query'), may hold values from 0 to 127
- targets: bfloat16 [3072, 8192], P('dp', 'query'), may hold values from -6 to 6
- w_one: bfloat16 [4096, 1024], P(None, 'query'), may hold values from -0.09375 to 0.09375
- b_one: float32 [1024], P('query'), may hold values from -3 to 3
- w_two: bfloat16 [1024, 512], P('query'), may hold values from -0.1875 to 0.1875
- b_two: float32 [512], replicated, may hold values from -3 to 3
- v_one: float32 [2, 512], replicated, may hold values from -4 to 4
- c_one: float32 [512], replicated, may hold values from -3 to 3
- v_two: bfloat16 [512, 512], replicated, may hold values from -0.25 to 0.25
- c_two: float32 [512], replicated, may hold values from -3 to 3
- v_three: bfloat16 [512, 512], replicated, may hold values from -0.25 to 0.25
- c_three: float32 [512], replicated, may hold values from -3 to 3
Outputs:
- loss: float32 [], replicated
- grad_w_one: float32 [4096, 1024], P('dp', 'query')
- grad_b_one: float32 [1024], P('query')
- grad_w_two: float32 [1024, 512], P('query', 'dp')
- grad_b_two: float32 [512], replicated
- grad_v_one: float32 [2, 512], replicated
- grad_c_one: float32 [512], replicated
- grad_v_two: float32 [512, 512], replicated
- grad_c_two: float32 [512], replicated
- grad_v_three: float32 [512, 512], replicated
- grad_c_three: float32 [512], replicated
All inputs are finite; a program needn't handle non-finite values.
Results may differ from a plain program's by a relative error of at most 0.00075.
Values may be sent and summed in bfloat16 or wider, within the bound.
A program may use at most 128 MiB of HBM per device.

v0:
```python
import math
import jax
import jax.numpy as jnp
from jax import lax
from jax.sharding import PartitionSpec as P

GRID = 128


def contract_rows(left, right, precision=None):
    return lax.dot_general(
        left,
        right,
        (((0,), (0,)), ((), ())),
        precision=precision,
        preferred_element_type=jnp.float32,
    )


def contract_cols(left, right, precision=None):
    return lax.dot_general(
        left,
        right,
        (((1,), (1,)), ((), ())),
        precision=precision,
        preferred_element_type=jnp.float32,
    )


def trunk_forward(coords, v_one, c_one, v_two, c_two, v_three, c_three):
    first_act = jnp.tanh(
        coords[0][:, None] * v_one[0][None, :] + coords[1][:, None] * v_one[1][None, :] + c_one
    )
    first_b = first_act.astype(jnp.bfloat16)
    second_act = jnp.tanh(jnp.dot(first_b, v_two, preferred_element_type=jnp.float32) + c_two)
    second_b = second_act.astype(jnp.bfloat16)
    basis_full = jnp.dot(second_b, v_three, preferred_element_type=jnp.float32) + c_three
    return (first_act, first_b, second_act, second_b, basis_full.astype(jnp.bfloat16))


def trunk_backward(coords, first_act, first_b, second_act, second_b, grad_basis, v_two, v_three):
    grad_basis_b = grad_basis.astype(jnp.bfloat16)
    grad_v_three = contract_rows(second_b, grad_basis_b)
    grad_c_three = jnp.sum(grad_basis, axis=0)
    grad_second = contract_cols(grad_basis_b, v_three) * (1.0 - second_act * second_act)
    grad_second_b = grad_second.astype(jnp.bfloat16)
    grad_v_two = contract_rows(first_b, grad_second_b)
    grad_c_two = jnp.sum(grad_second, axis=0)
    grad_first = contract_cols(grad_second_b, v_two) * (1.0 - first_act * first_act)
    grad_v_one = jnp.dot(
        coords, grad_first, precision=lax.Precision.HIGHEST, preferred_element_type=jnp.float32
    )
    grad_c_one = jnp.sum(grad_first, axis=0)
    return (grad_v_one, grad_c_one, grad_v_two, grad_c_two, grad_v_three, grad_c_three)


def local(
    sensors,
    query_index,
    targets,
    w_one,
    b_one,
    w_two,
    b_two,
    v_one,
    c_one,
    v_two,
    c_two,
    v_three,
    c_three,
):
    dp_count = lax.axis_size("dp")
    func_rows = sensors.shape[0]
    query_rows = query_index.shape[1]
    count_all = func_rows * dp_count * query_rows * lax.axis_size("query")
    grad_scale = 64.0 / math.sqrt(count_all)
    inv_scale = 1.0 / math.sqrt(w_two.shape[1])
    coords_all = query_index.astype(jnp.float32) / (GRID - 1)
    hidden = jnp.tanh(jnp.dot(sensors, w_one, preferred_element_type=jnp.float32) + b_one)
    hidden_b = hidden.astype(jnp.bfloat16)
    partial_value = jnp.dot(hidden_b, w_two, preferred_element_type=jnp.float32)
    coeffs = lax.psum(partial_value, "query") + b_two
    coeffs_b = coeffs.astype(jnp.bfloat16)
    row_share = query_rows // dp_count
    coords_mine = lax.dynamic_slice_in_dim(
        coords_all, lax.axis_index("dp") * row_share, row_share, 1
    )
    first_act, first_b, second_act, second_b, basis_b = trunk_forward(
        coords_mine, v_one, c_one, v_two, c_two, v_three, c_three
    )
    basis_all = lax.all_gather(basis_b, "dp", axis=0, tiled=True)
    prediction = contract_cols(coeffs_b, basis_all) * inv_scale
    misfit = prediction - targets.astype(jnp.float32)
    loss_part = jnp.sum(misfit * misfit)
    misfit_b = (misfit * grad_scale).astype(jnp.bfloat16)
    grad_coeffs = lax.psum(
        jnp.dot(misfit_b, basis_all, preferred_element_type=jnp.float32) * inv_scale, "query"
    )
    grad_coeffs_b = grad_coeffs.astype(jnp.bfloat16)
    loss_value = lax.psum(loss_part, ("dp", "query")) / count_all
    columns = misfit_b
    grad_basis = lax.psum_scatter(
        contract_rows(columns, coeffs_b) * inv_scale, "dp", scatter_dimension=0, tiled=True
    )
    trunk_parts = trunk_backward(
        coords_mine, first_act, first_b, second_act, second_b, grad_basis, v_two, v_three
    )
    grad_w_two_part = contract_rows(hidden_b, grad_coeffs_b)
    grad_pre = contract_cols(grad_coeffs_b, w_two) * (1.0 - hidden * hidden)
    grad_pre_b = grad_pre.astype(jnp.bfloat16)
    grad_b_one, grad_b_two = lax.psum(
        (jnp.sum(grad_pre, axis=0), jnp.sum(grad_coeffs, axis=0)), "dp"
    )
    columns = sensors
    grad_w_one = lax.psum_scatter(
        contract_rows(columns, grad_pre_b), "dp", scatter_dimension=0, tiled=True
    )
    grad_w_two = lax.psum_scatter(grad_w_two_part, "dp", scatter_dimension=1, tiled=True)
    trunk_sums = lax.psum(
        (
            trunk_parts[0],
            trunk_parts[1],
            trunk_parts[2],
            trunk_parts[3],
            trunk_parts[4],
            trunk_parts[5],
        ),
        ("dp", "query"),
    )
    return (
        loss_value,
        grad_w_one,
        grad_b_one,
        grad_w_two,
        grad_b_two,
        trunk_sums[0],
        trunk_sums[1],
        trunk_sums[2],
        trunk_sums[3],
        trunk_sums[4],
        trunk_sums[5],
    )


def solution(mesh):
    placed = (
        P("dp", None),
        P(None, "query"),
        P("dp", "query"),
        P(None, "query"),
        P("query"),
        P("query", None),
        P(),
        P(),
        P(),
        P(),
        P(),
        P(),
        P(),
    )
    return jax.shard_map(
        local,
        mesh=mesh,
        in_specs=placed,
        out_specs=(
            P(),
            P("dp", "query"),
            P("query"),
            P("query", "dp"),
            P(),
            P(),
            P(),
            P(),
            P(),
            P(),
            P(),
        ),
        check_vma=False,
    )
```

profile of v0, /device:TPU:0, one launch (start us, length us, event | category | flops | bytes accessed | tf_op | source)
XLA Modules:
  0.0 356.2 jit_solution(2929589968027508688)
XLA Ops:
  8.1 1.8 copy-done
  9.9 2.6 fusion.2
  17.5 2.1 fusion.1
  19.6 32.0 %all-reduce.7.cloned.1.call-done = f32[384,512]{1,0:T(8,128)} async-done(((f32[384,512]{1,0:T(8,128)}), f32[384,512]{1,0:T(8,128)}) %all-reduce.7.cloned.1.call-update) | async-done | bytes 786448 | tf_op jit(solution)/shard_map/psum | solution.py:82
  51.6 19.8 %all-gather.2.cloned.1.call-done = bf16[2048,512]{1,0:T(8,128)(2,1)} async-done(((bf16[256,512]{1,0:T(8,128)(2,1)}), bf16[2048,512]{1,0:T(8,128)(2,1)}) %all-gather.2.cloned.1.call-update) | async-done | bytes 2097168 | tf_op jit(solution)/shard_map/all_gather | solution.py:91
  71.4 4.2 %multiply_reduce_fusion = (f32[]{:T(128)}, f32[384,2048]{1,0:T(8,128)S(1)}) fusion(bf16[384,2048]{1,0:T(8,128)(2,1)} %param.15, bf16[2048,512]{1,0:T(8,128)(2,1)} %all-gather.2.cloned.1.call-done, f32[384,512]{1,0:T(8,128)} %all-reduce.7.cloned.1.call-done, f32[512]{0:T(512)S(1)} %copy-done.7), kind=kOutput, calls=%fused_computation.3 | convolution fusion | flops 809631744 | bytes 7604228 | tf_op jit(solution)/shard_map/dot_general | solution.py:21
  75.6 1.6 copy-done.1
  77.2 1.9 convolution_multiply_fusion.1
  79.2 5.3 %convolution_multiply_fusion = f32[2048,512]{1,0:T(8,128)} fusion(f32[384,2048]{1,0:T(8,128)} %copy-done.1, f32[384,512]{1,0:T(8,128)} %all-reduce.7.cloned.1.call-done, f32[512]{0:T(512)S(1)} %copy-done.7), kind=kOutput, calls=%fused_computation.1 | convolution fusion | flops 808321024 | bytes 8128512 | tf_op jit(solution)/shard_map/dot_general | solution.py:11
  84.6 28.1 %all-reduce.9.cloned.1.call-done = f32[384,512]{1,0:T(8,128)} async-done(((f32[384,512]{1,0:T(8,128)}), f32[384,512]{1,0:T(8,128)}) %all-reduce.9.cloned.1.call-update) | async-done | bytes 786448 | tf_op jit(solution)/shard_map/psum | solution.py:96
  112.8 2.1 fusion.28
  114.8 3.2 convolution_bitcast_fusion
  118.1 2.3 fusion.8
  120.5 51.0 %reduce-scatter.8.cloned.1.call-done = f32[256,512]{1,0:T(8,128)} async-done(((f32[2048,512]{1,0:T(8,128)}), f32[256,512]{1,0:T(8,128)}) %reduce-scatter.8.cloned.1.call-update) | async-done | bytes 524304 | tf_op jit(solution)/shard_map/reduce_scatter | solution.py:102
  171.5 1.8 fusion.27
  173.3 2.2 fusion.4
  178.0 21.5 %all-reduce.2 = (f32[256]{0:T(256)}, f32[512]{0:T(512)}) all-reduce(f32[256]{0:T(256)S(1)} %copy-done.12, f32[512]{0:T(512)S(1)} %reduce_sum.56), channel_id=1, replica_groups=mesh['dp'=8,'query'=4] {'dp'}, use_global_device_ids=true, to_apply=%region_6.0 | all-reduce | flops 768 | bytes 6144 | tf_op jit(solution)/shard_map/psum | solution.py:111
  202.5 38.7 %all-reduce = (f32[]{:T(128)}, f32[2,512]{1,0:T(2,128)}, f32[512]{0:T(512)}, f32[512]{0:T(512)}, f32[512]{0:T(512)}) all-reduce(f32[]{:T(128)} %get-tuple-element.35, f32[2,512]{1,0:T(2,128)S(1)} %fusion.29, f32[512]{0:T(512)S(1)} %get-tuple-element.37, ...), channel_id=1, replica_groups=mesh['dp'=8,'query'=4] {'dp','query'}, use_global_device_ids=true, to_apply=%region_2.0 | all-reduce | flops 2561 | bytes 20488 | tf_op jit(solution)/shard_map/psum | solution.py:100
  241.8 31.0 %reduce-scatter.4.cloned.1.call-done = f32[512,256]{0,1:T(8,128)} async-done(((f32[4096,256]{0,1:T(8,128)}), f32[512,256]{0,1:T(8,128)}) %reduce-scatter.4.cloned.1.call-update) | async-done | bytes 524304 | tf_op jit(solution)/shard_map/reduce_scatter | solution.py:115
  272.8 2.0 copy.24
  274.8 64.7 %reduce-scatter.6.cloned.1.call-done = f32[256,64]{0,1:T(8,128)} async-done(((f32[256,512]{0,1:T(8,128)}), f32[256,64]{0,1:T(8,128)}) %reduce-scatter.6.cloned.1.call-update) | async-done | bytes 65552 | tf_op jit(solution)/shard_map/reduce_scatter | solution.py:118
  339.5 3.7 %all-reduce.11.cloned.1.call-done = (f32[512,512]{1,0:T(8,128)}, f32[512,512]{1,0:T(8,128)}) async-done(((f32[512,512]{1,0:T(8,128)}, f32[512,512]{1,0:T(8,128)}), (f32[512,512]{1,0:T(8,128)}, f32[512,512]{1,0:T(8,128)})) %all-reduce.11.cloned.1.call-update) | async-done | bytes 2097168 | tf_op jit(solution)/shard_map/psum | solution.py:119
  343.2 2.3 copy.29
  345.5 2.3 copy.30
  (50 shorter events, 10.7 us)
Async XLA Ops:
  8.0 1.9 copy-start
  8.0 43.6 %all-reduce.7.cloned.1.call-start = ((), (), s32[]{:S(2)}) async-start(), calls=%async_computation.3 | async-start | bytes 1572864 | tf_op jit(solution)/shard_map/psum | solution.py:82
  9.9 2.6 copy-start.6
  12.5 58.9 %copy-start.7 = (f32[512]{0:T(512)S(1)}, f32[512]{0:T(512)}, u32[]{:S(2)}) copy-start(f32[512]{0:T(512)} %param.19) | copy-start | bytes 6148
  13.7 57.7 %all-gather.2.cloned.1.call-start = ((), (), s32[]{:S(2)}) async-start(), calls=%async_computation.4 | async-start | bytes 2359296 | tf_op jit(solution)/shard_map/all_gather | solution.py:91
  14.5 0.8 copy-start.8
  14.5 2.2 copy-start.10
  16.7 0.8 copy-start.2
  19.6 93.2 %all-reduce.9.cloned.1.call-start = ((), (), s32[]{:S(2)}) async-start(), calls=%async_computation.5 | async-start | bytes 1572864 | tf_op jit(solution)/shard_map/psum | solution.py:96
  71.4 5.8 %copy-start.5 = (bf16[2048,512]{1,0:T(8,128)(2,1)S(1)}, bf16[2048,512]{1,0:T(8,128)(2,1)}, u32[]{:S(2)}) copy-start(bf16[2048,512]{1,0:T(8,128)(2,1)} %all-gather.2.cloned.1.call-done) | copy-start | bytes 6291460
  75.6 1.6 copy-start.1
  79.1 92.3 %reduce-scatter.8.cloned.1.call-start = ((), (), s32[]{:S(2)}) async-start(), calls=%async_computation.8 | async-start | bytes 4718592 | tf_op jit(solution)/shard_map/reduce_scatter | solution.py:102
  84.5 188.2 %reduce-scatter.4.cloned.1.call-start = ((), (), s32[]{:S(2)}) async-start(), calls=%async_computation.6 | async-start | bytes 4718592 | tf_op jit(solution)/shard_map/reduce_scatter | solution.py:115
  118.0 55.2 %copy-start.9 = (f32[1,256]{1,0:T(1,128)S(1)}, f32[1,256]{1,0:T(1,128)}, u32[]{:S(2)}) copy-start(f32[1,256]{1,0:T(1,128)} %copy-done.8) | copy-start | bytes 3076
  118.1 221.4 %reduce-scatter.6.cloned.1.call-start = ((), (), s32[]{:S(2)}) async-start(), calls=%async_computation.7 | async-start | bytes 589824 | tf_op jit(solution)/shard_map/reduce_scatter | solution.py:118
  120.4 222.8 %all-reduce.11.cloned.1.call-start = ((), (), s32[]{:S(2)}) async-start(), calls=%async_computation.9 | async-start | bytes 4194304 | tf_op jit(solution)/shard_map/psum | solution.py:119
  171.5 4.0 %copy-start.3 = (f32[256,512]{1,0:T(8,128)S(1)}, f32[256,512]{1,0:T(8,128)}, u32[]{:S(2)}) copy-start(f32[256,512]{1,0:T(8,128)} %copy-done.2) | copy-start | bytes 1572868
  171.5 4.0 %copy-start.4 = (f32[256,512]{1,0:T(8,128)S(1)}, f32[256,512]{1,0:T(8,128)}, u32[]{:S(2)}) copy-start(f32[256,512]{1,0:T(8,128)} %reduce-scatter.8.cloned.1.call-done) | copy-start | bytes 1572868
  173.3 4.8 %copy-start.12 = (f32[256]{0:T(256)S(1)}, f32[256]{0:T(256)}, u32[]{:S(2)}) copy-start(f32[256]{0:T(256)} %get-tuple-element.41) | copy-start | bytes 3076
  173.3 27.4 %copy-start.11 = (f32[1,256]{1,0:T(1,128)S(1)}, f32[1,256]{1,0:T(1,128)}, u32[]{:S(2)}) copy-start(f32[1,256]{1,0:T(1,128)} %copy-done.10) | copy-start | bytes 3076
  173.3 27.4 %copy-start.13 = (f32[512]{0:T(512)S(1)}, f32[512]{0:T(512)}, u32[]{:S(2)}) copy-start(f32[512]{0:T(512)} %param.21) | copy-start | bytes 6148
Sparse Core Ops, SparseCore 0:
  13.9 37.7 all-reduce.6
  79.2 33.4 all-reduce.8
  176.9 166.2 all-reduce.10
Sparse Core Ops, SparseCore 1:
  19.7 51.7 all-gather.1
  84.6 86.8 reduce-scatter.7
  175.0 97.7 reduce-scatter.3
  276.7 62.7 reduce-scatter.5
where the time goes:
time: 357 us; the launch traced here: 356 us
  waiting for transfers between devices  230 us (64%)
  blocking collectives  60.2 us (17%)
  matrix products  33.3 us (9%)
  between operations  17.4 us (5%)
  local copies, waits for them, and re-layouts  11.7 us (3%)
    reduce_scatter x1, waiting for transfers between devices, local(): lax.psum_scatter(grad_w_two_part, 'dp', scatter_dimension=1, tiled=True)  64.7 us
    reduce_scatter x1, waiting for transfers between devices, local(): lax.psum_scatter(contract_rows(columns, coeffs_b) * inv_scale, 'dp', scat...  51 us
    psum x1, blocking collectives, local(): loss_value = lax.psum(loss_part, ('dp', 'query')) / count_all  38.7 us
    psum x1, waiting for transfers between devices, local(): coeffs = lax.psum(partial_value, 'query') + b_two  32 us
    reduce_scatter x1, waiting for transfers between devices, local(): lax.psum_scatter(contract_rows(columns, grad_pre_b), 'dp', scatter_dimens...  31 us
    psum x1, waiting for transfers between devices, local(): lax.psum(jnp.dot(misfit_b, basis_all, preferred_element_type=jnp.float32)...  28.1 us
    psum x1, blocking collectives, local(): lax.psum((jnp.sum(grad_pre, axis=0), jnp.sum(grad_coeffs, axis=0)), 'dp')  21.5 us
    all_gather x1, waiting for transfers between devices, local(): basis_all = lax.all_gather(basis_b, 'dp', axis=0, tiled=True)  19.8 us
  transfers between devices with their start and end apart: 7, of which 7 were waited for; matrix products, arithmetic and copies ran while one was open for 8% of the time, Pallas kernels for 0%

commit v1 on v0

--- a/solution.py
+++ b/solution.py
@@ -88,7 +88,12 @@
     first_act, first_b, second_act, second_b, basis_b = trunk_forward(
         coords_mine, v_one, c_one, v_two, c_two, v_three, c_three
     )
-    basis_all = lax.all_gather(basis_b, "dp", axis=0, tiled=True)
+    ring = [basis_b]
+    for hop in range(7):
+        ring.append(lax.ppermute(ring[-1], "dp", [(dev, (dev + 1) % 8) for dev in range(8)]))
+    basis_all = jnp.roll(
+        jnp.concatenate(ring[::-1], axis=0), (lax.axis_index("dp") + 1) * ring[0].shape[0], axis=0
+    )
     prediction = contract_cols(coeffs_b, basis_all) * inv_scale
     misfit = prediction - targets.astype(jnp.float32)
     loss_part = jnp.sum(misfit * misfit)

time: 357 us -> 561 us (1.57)
  waiting for transfers between devices: 230 us -> 412 us
  local copies, waits for them, and re-layouts: 11.7 us -> 31.1 us
    psum x1, waiting for transfers between devices: 3.7 us -> 140 us  [local(): lax.psum((trunk_parts[0], trunk_parts[1], trunk_parts[2], trunk_parts[3],...]
    ppermute x0 -> x7, waiting for transfers between devices: none -> 61.8 us  [local(): lax.ppermute(ring[-1], 'dp', [(dev, (dev + 1) % 8) for dev in range(8)])]
    reduce_scatter x1, waiting for transfers between devices: 51 us -> 84.2 us  [local(): lax.psum_scatter(contract_rows(columns, coeffs_b) * inv_scale, 'dp', scat...]
    psum x1, waiting for transfers between devices: 32 us -> 9.63 us  [local(): coeffs = lax.psum(partial_value, 'query') + b_two]
    all_gather x1 -> x0, waiting for transfers between devices: 19.8 us -> none  [local(): basis_all = lax.all_gather(basis_b, 'dp', axis=0, tiled=True)]
    unnamed x31 -> x64, local copies, waits for them, and re-layouts: 10.9 us -> 29.6 us
    reduce_scatter x1, waiting for transfers between devices: 31 us -> 22.4 us  [local(): lax.psum_scatter(contract_rows(columns, grad_pre_b), 'dp', scatter_dimens...]
  transfers between devices with their start and end apart: 7 -> 13, of which waited for: 7 -> 13; matrix products, arithmetic and copies ran while one was open for 8% -> 9% of each run, Pallas kernels for 0% -> 0%
where the time goes in v1:
time: 561 us; the launch traced here: 560 us
  waiting for transfers between devices  412 us (73%)
  blocking collectives  58.8 us (10%)
  matrix products  35.1 us (6%)
  local copies, waits for them, and re-layouts  31.1 us (6%)
  between operations  16.2 us (3%)
    psum x1, waiting for transfers between devices, local(): lax.psum((trunk_parts[0], trunk_parts[1], trunk_parts[2], trunk_parts[3],...  140 us
    reduce_scatter x1, waiting for transfers between devices, local(): lax.psum_scatter(contract_rows(columns, coeffs_b) * inv_scale, 'dp', scat...  84.2 us
    reduce_scatter x1, waiting for transfers between devices, local(): lax.psum_scatter(grad_w_two_part, 'dp', scatter_dimension=1, tiled=True)  64 us
    ppermute x7, waiting for transfers between devices, local(): lax.ppermute(ring[-1], 'dp', [(dev, (dev + 1) % 8) for dev in range(8)])  61.8 us
    psum x1, blocking collectives, local(): loss_value = lax.psum(loss_part, ('dp', 'query')) / count_all  37.1 us
    psum x1, waiting for transfers between devices, local(): lax.psum(jnp.dot(misfit_b, basis_all, preferred_element_type=jnp.float32)...  29.7 us
    unnamed x64, local copies, waits for them, and re-layouts  29.6 us
    reduce_scatter x1, waiting for transfers between devices, local(): lax.psum_scatter(contract_rows(columns, grad_pre_b), 'dp', scatter_dimens...  22.4 us
  transfers between devices with their start and end apart: 13, of which 13 were waited for; matrix products, arithmetic and copies ran while one was open for 9% of the time, Pallas kernels for 0%

profile of v1, /device:TPU:0, one launch (start us, length us, event | category | flops | bytes accessed | tf_op | source)
XLA Modules:
  0.0 559.5 jit_solution(1735398359762262196)
XLA Ops:
  12.5 3.0 collective-permute-start
  15.6 9.3 %collective-permute-done = bf16[256,512]{1,0:T(8,128)(2,1)S(1)} collective-permute-done((bf16[256,512]{1,0:T(8,128)(2,1)S(1)}, bf16[256,512]{1,0:T(8,128)(2,1)S(1)}, u32[]{:S(2)}, u32[]{:S(2)}) %collective-permute-start) | collective-permute-done | bytes 262176 | tf_op jit(solution)/shard_map/ppermute | solution.py:93
  24.9 10.2 %collective-permute-done.1 = bf16[256,512]{1,0:T(8,128)(2,1)S(1)} collective-permute-done((bf16[256,512]{1,0:T(8,128)(2,1)S(1)}, bf16[256,512]{1,0:T(8,128)(2,1)S(1)}, u32[]{:S(2)}, u32[]{:S(2)}) %collective-permute-start.1) | collective-permute-done | bytes 262176 | tf_op jit(solution)/shard_map/ppermute | solution.py:93
  35.1 9.3 %collective-permute-done.2 = bf16[256,512]{1,0:T(8,128)(2,1)S(1)} collective-permute-done((bf16[256,512]{1,0:T(8,128)(2,1)S(1)}, bf16[256,512]{1,0:T(8,128)(2,1)S(1)}, u32[]{:S(2)}, u32[]{:S(2)}) %collective-permute-start.2) | collective-permute-done | bytes 262176 | tf_op jit(solution)/shard_map/ppermute | solution.py:93
  44.4 9.1 %collective-permute-done.3 = bf16[256,512]{1,0:T(8,128)(2,1)S(1)} collective-permute-done((bf16[256,512]{1,0:T(8,128)(2,1)S(1)}, bf16[256,512]{1,0:T(8,128)(2,1)S(1)}, u32[]{:S(2)}, u32[]{:S(2)}) %collective-permute-start.3) | collective-permute-done | bytes 262176 | tf_op jit(solution)/shard_map/ppermute | solution.py:93
  53.5 9.1 %collective-permute-done.4 = bf16[256,512]{1,0:T(8,128)(2,1)S(1)} collective-permute-done((bf16[256,512]{1,0:T(8,128)(2,1)S(1)}, bf16[256,512]{1,0:T(8,128)(2,1)S(1)}, u32[]{:S(2)}, u32[]{:S(2)}) %collective-permute-start.4) | collective-permute-done | bytes 262176 | tf_op jit(solution)/shard_map/ppermute | solution.py:93
  62.5 9.4 %collective-permute-done.5 = bf16[256,512]{1,0:T(8,128)(2,1)} collective-permute-done((bf16[256,512]{1,0:T(8,128)(2,1)S(1)}, bf16[256,512]{1,0:T(8,128)(2,1)}, u32[]{:S(2)}, u32[]{:S(2)}) %collective-permute-start.5) | collective-permute-done | bytes 262176 | tf_op jit(solution)/shard_map/ppermute | solution.py:93
  72.0 2.6 fusion.8
  75.9 5.5 collective-permute-done.6
  102.5 9.6 %all-reduce.7.cloned.1.call-done = f32[384,512]{1,0:T(8,128)} async-done(((f32[384,512]{1,0:T(8,128)}), f32[384,512]{1,0:T(8,128)}) %all-reduce.7.cloned.1.call-update) | async-done | bytes 786448 | tf_op jit(solution)/shard_map/psum | solution.py:82
  112.2 4.0 multiply_reduce_fusion
  117.9 3.5 fusion.3
  121.5 5.4 convolution_multiply_fusion
  126.9 29.7 %all-reduce.9.cloned.1.call-done = f32[384,512]{1,0:T(8,128)} async-done(((f32[384,512]{1,0:T(8,128)}), f32[384,512]{1,0:T(8,128)}) %all-reduce.9.cloned.1.call-update) | async-done | bytes 786448 | tf_op jit(solution)/shard_map/psum | solution.py:101
  158.6 3.2 convolution_bitcast_fusion
  162.0 2.3 fusion.14
  164.4 84.2 %reduce-scatter.8.cloned.1.call-done = f32[256,512]{1,0:T(8,128)} async-done(((f32[2048,512]{1,0:T(8,128)}), f32[256,512]{1,0:T(8,128)}) %reduce-scatter.8.cloned.1.call-update) | async-done | bytes 524304 | tf_op jit(solution)/shard_map/reduce_scatter | solution.py:107
  252.4 2.5 fusion.19
  256.1 21.7 %all-reduce.2 = (f32[256]{0:T(256)}, f32[512]{0:T(512)}) all-reduce(f32[256]{0:T(256)S(1)} %copy-done.21, f32[512]{0:T(512)S(1)} %reduce_sum.56), channel_id=1, replica_groups=mesh['dp'=8,'query'=4] {'dp'}, use_global_device_ids=true, to_apply=%region_6.7 | all-reduce | flops 768 | bytes 6144 | tf_op jit(solution)/shard_map/psum | solution.py:116
  280.7 37.1 %all-reduce = (f32[]{:T(128)}, f32[2,512]{1,0:T(2,128)}, f32[512]{0:T(512)}, f32[512]{0:T(512)}, f32[512]{0:T(512)}) all-reduce(f32[]{:T(128)} %get-tuple-element.35, f32[2,512]{1,0:T(2,128)S(1)} %fusion.37, f32[512]{0:T(512)S(1)} %get-tuple-element.37, ...), channel_id=1, replica_groups=mesh['dp'=8,'query'=4] {'dp','query'}, use_global_device_ids=true, to_apply=%region_2.3 | all-reduce | flops 2561 | bytes 20488 | tf_op jit(solution)/shard_map/psum | solution.py:105
  318.5 22.4 %reduce-scatter.4.cloned.1.call-done = f32[512,256]{0,1:T(8,128)} async-done(((f32[4096,256]{0,1:T(8,128)}), f32[512,256]{0,1:T(8,128)}) %reduce-scatter.4.cloned.1.call-update) | async-done | bytes 524304 | tf_op jit(solution)/shard_map/reduce_scatter | solution.py:120
  342.9 64.0 %reduce-scatter.6.cloned.1.call-done = f32[256,64]{0,1:T(8,128)} async-done(((f32[256,512]{0,1:T(8,128)}), f32[256,64]{0,1:T(8,128)}) %reduce-scatter.6.cloned.1.call-update) | async-done | bytes 65552 | tf_op jit(solution)/shard_map/reduce_scatter | solution.py:123
  406.9 140.1 %all-reduce.11.cloned.1.call-done = (f32[512,512]{1,0:T(8,128)}, f32[512,512]{1,0:T(8,128)}) async-done(((f32[512,512]{1,0:T(8,128)}, f32[512,512]{1,0:T(8,128)}), (f32[512,512]{1,0:T(8,128)}, f32[512,512]{1,0:T(8,128)})) %all-reduce.11.cloned.1.call-update) | async-done | bytes 2097168 | tf_op jit(solution)/shard_map/psum | solution.py:124
  547.0 2.3 copy.44
  (95 shorter events, 44.0 us)
Async XLA Ops:
  7.2 64.9 %copy-start = (bf16[384,4096]{1,0:T(8,128)(2,1)S(1)}, bf16[384,4096]{1,0:T(8,128)(2,1)}, u32[]{:S(2)}) copy-start(bf16[384,4096]{1,0:T(8,128)(2,1)} %param.13) | copy-start | bytes 9437188
  7.2 105.0 %all-reduce.7.cloned.1.call-start = ((), (), s32[]{:S(2)}) async-start(), calls=%async_computation.3 | async-start | bytes 1572864 | tf_op jit(solution)/shard_map/psum | solution.py:82
  11.1 63.5 %copy-start.15 = (bf16[256,512]{1,0:T(8,128)(2,1)S(1)}, bf16[256,512]{1,0:T(8,128)(2,1)}, u32[]{:S(2)}) copy-start(bf16[256,512]{1,0:T(8,128)(2,1)} %param.18) | copy-start | bytes 786436
  12.5 59.4 %copy-start.3 = (bf16[256,512]{1,0:T(8,128)(2,1)}, bf16[256,512]{1,0:T(8,128)(2,1)S(1)}, u32[]{:S(2)}) copy-start(bf16[256,512]{1,0:T(8,128)(2,1)S(1)} %fusion.7) | copy-start | bytes 786436
  12.5 12.4 %collective-permute-start = (bf16[256,512]{1,0:T(8,128)(2,1)S(1)}, bf16[256,512]{1,0:T(8,128)(2,1)S(1)}, u32[]{:S(2)}, u32[]{:S(2)}) collective-permute-start(bf16[256,512]{1,0:T(8,128)(2,1)S(1)} %fusion.7), channel_id=1, source_target_pairs={{0,4},{4,8},{8,12},{12,16},{16,20},{20,24},{24,28},{28,0},{1,5},{5... | collective-permute-start | bytes 786440 | tf_op jit(solution)/shard_map/ppermute | solution.py:93
  24.9 47.0 %copy-start.5 = (bf16[256,512]{1,0:T(8,128)(2,1)}, bf16[256,512]{1,0:T(8,128)(2,1)S(1)}, u32[]{:S(2)}) copy-start(bf16[256,512]{1,0:T(8,128)(2,1)S(1)} %collective-permute-done) | copy-start | bytes 786436
  24.9 10.2 %collective-permute-start.1 = (bf16[256,512]{1,0:T(8,128)(2,1)S(1)}, bf16[256,512]{1,0:T(8,128)(2,1)S(1)}, u32[]{:S(2)}, u32[]{:S(2)}) collective-permute-start(bf16[256,512]{1,0:T(8,128)(2,1)S(1)} %collective-permute-done), channel_id=1, source_target_pairs={{0,4},{4,8},{8,12},{12,16},{16,20},{20,24},{24,28},{28,0},{1,5},{5... | collective-permute-start | bytes 786440 | tf_op jit(solution)/shard_map/ppermute | solution.py:93
  35.1 36.8 %copy-start.7 = (bf16[256,512]{1,0:T(8,128)(2,1)}, bf16[256,512]{1,0:T(8,128)(2,1)S(1)}, u32[]{:S(2)}) copy-start(bf16[256,512]{1,0:T(8,128)(2,1)S(1)} %collective-permute-done.1) | copy-start | bytes 786436
  35.1 9.3 %collective-permute-start.2 = (bf16[256,512]{1,0:T(8,128)(2,1)S(1)}, bf16[256,512]{1,0:T(8,128)(2,1)S(1)}, u32[]{:S(2)}, u32[]{:S(2)}) collective-permute-start(bf16[256,512]{1,0:T(8,128)(2,1)S(1)} %collective-permute-done.1), channel_id=1, source_target_pairs={{0,4},{4,8},{8,12},{12,16},{16,20},{20,24},{24,28},{28,0},{1,5},{5... | collective-permute-start | bytes 786440 | tf_op jit(solution)/shard_map/ppermute | solution.py:93
  44.4 27.5 %copy-start.9 = (bf16[256,512]{1,0:T(8,128)(2,1)}, bf16[256,512]{1,0:T(8,128)(2,1)S(1)}, u32[]{:S(2)}) copy-start(bf16[256,512]{1,0:T(8,128)(2,1)S(1)} %collective-permute-done.2) | copy-start | bytes 786436
  44.4 9.1 %collective-permute-start.3 = (bf16[256,512]{1,0:T(8,128)(2,1)S(1)}, bf16[256,512]{1,0:T(8,128)(2,1)S(1)}, u32[]{:S(2)}, u32[]{:S(2)}) collective-permute-start(bf16[256,512]{1,0:T(8,128)(2,1)S(1)} %collective-permute-done.2), channel_id=1, source_target_pairs={{0,4},{4,8},{8,12},{12,16},{16,20},{20,24},{24,28},{28,0},{1,5},{5... | collective-permute-start | bytes 786440 | tf_op jit(solution)/shard_map/ppermute | solution.py:93
  53.5 9.1 %collective-permute-start.4 = (bf16[256,512]{1,0:T(8,128)(2,1)S(1)}, bf16[256,512]{1,0:T(8,128)(2,1)S(1)}, u32[]{:S(2)}, u32[]{:S(2)}) collective-permute-start(bf16[256,512]{1,0:T(8,128)(2,1)S(1)} %collective-permute-done.3), channel_id=1, source_target_pairs={{0,4},{4,8},{8,12},{12,16},{16,20},{20,24},{24,28},{28,0},{1,5},{5... | collective-permute-start | bytes 786440 | tf_op jit(solution)/shard_map/ppermute | solution.py:93
  62.5 9.4 %collective-permute-start.5 = (bf16[256,512]{1,0:T(8,128)(2,1)S(1)}, bf16[256,512]{1,0:T(8,128)(2,1)}, u32[]{:S(2)}, u32[]{:S(2)}) collective-permute-start(bf16[256,512]{1,0:T(8,128)(2,1)S(1)} %collective-permute-done.4), channel_id=1, source_target_pairs={{0,4},{4,8},{8,12},{12,16},{16,20},{20,24},{24,28},{28,0},{1,5},{5... | collective-permute-start | bytes 786440 | tf_op jit(solution)/shard_map/ppermute | solution.py:93
  72.0 9.4 %collective-permute-start.6 = (bf16[256,512]{1,0:T(8,128)(2,1)}, bf16[256,512]{1,0:T(8,128)(2,1)}, u32[]{:S(2)}, u32[]{:S(2)}) collective-permute-start(bf16[256,512]{1,0:T(8,128)(2,1)} %collective-permute-done.5), channel_id=1, source_target_pairs={{0,4},{4,8},{8,12},{12,16},{16,20},{20,24},{24,28},{28,0},{1,5},{5... | collective-permute-start | bytes 786440 | tf_op jit(solution)/shard_map/ppermute | solution.py:93
  75.8 80.8 %all-reduce.9.cloned.1.call-start = ((), (), s32[]{:S(2)}) async-start(), calls=%async_computation.4 | async-start | bytes 1572864 | tf_op jit(solution)/shard_map/psum | solution.py:101
  75.9 36.2 %copy-start.16 = (f32[512]{0:T(512)S(1)}, f32[512]{0:T(512)}, u32[]{:S(2)}) copy-start(f32[512]{0:T(512)} %param.19) | copy-start | bytes 6148
  121.4 127.1 %reduce-scatter.8.cloned.1.call-start = ((), (), s32[]{:S(2)}) async-start(), calls=%async_computation.7 | async-start | bytes 4718592 | tf_op jit(solution)/shard_map/reduce_scatter | solution.py:107
  126.8 214.0 %reduce-scatter.4.cloned.1.call-start = ((), (), s32[]{:S(2)}) async-start(), calls=%async_computation.5 | async-start | bytes 4718592 | tf_op jit(solution)/shard_map/reduce_scatter | solution.py:120
  161.9 88.3 %copy-start.18 = (f32[1,256]{1,0:T(1,128)S(1)}, f32[1,256]{1,0:T(1,128)}, u32[]{:S(2)}) copy-start(f32[1,256]{1,0:T(1,128)} %copy-done.17) | copy-start | bytes 3076
  161.9 245.0 %reduce-scatter.6.cloned.1.call-start = ((), (), s32[]{:S(2)}) async-start(), calls=%async_computation.6 | async-start | bytes 589824 | tf_op jit(solution)/shard_map/reduce_scatter | solution.py:123
  164.3 91.8 %copy-start.21 = (f32[256]{0:T(256)S(1)}, f32[256]{0:T(256)}, u32[]{:S(2)}) copy-start(f32[256]{0:T(256)} %get-tuple-element.41) | copy-start | bytes 3076
  164.3 114.6 %copy-start.20 = (f32[1,256]{1,0:T(1,128)S(1)}, f32[1,256]{1,0:T(1,128)}, u32[]{:S(2)}) copy-start(f32[1,256]{1,0:T(1,128)} %copy-done.19) | copy-start | bytes 3076
  164.3 114.6 %copy-start.22 = (f32[512]{0:T(512)S(1)}, f32[512]{0:T(512)}, u32[]{:S(2)}) copy-start(f32[512]{0:T(512)} %param.21) | copy-start | bytes 6148
  164.3 382.7 %all-reduce.11.cloned.1.call-start = ((), (), s32[]{:S(2)}) async-start(), calls=%async_computation.8 | async-start | bytes 4194304 | tf_op jit(solution)/shard_map/psum | solution.py:124
  (12 other events, 176.7 us)
Sparse Core Ops, SparseCore 0:
  75.9 36.2 all-reduce.6
  121.5 35.0 all-reduce.8
  160.2 88.2 reduce-scatter.7
  252.0 88.7 reduce-scatter.3
  344.6 62.2 reduce-scatter.5
  413.4 133.5 all-reduce.10
